TPU v7x, 32 devices: a whole 2x2x4 slice. The times are simulated.
32 devices in a mesh: rep: 2 (over x), shard: 16 (over z, y, core).
Axes of the slice: x: 2, y: 2, z: 4, core: 2. Of those that a mesh axis runs over, the one named last changes fastest.
Arguments:
- tokens_x: bfloat16 [8192, 4096], P(('rep', 'shard')), may hold values from -6 to 6
- key_grad: bfloat16 [8192, 1024], P(('rep', 'shard')), may hold values from -0.06591797 to 0.06591797
- left_root: bfloat16 [64, 512, 512], P('shard'), may hold values from -1 to 3
- slot_grads: bfloat16 [64, 512, 512], P('shard'), may hold values from -6 to 6
- right_root: bfloat16 [64, 512, 512], P('shard'), may hold values from -1 to 3
- block_slot: int32 [32], replicated, may hold values from 0 to 63, as said below
Outputs:
- grad_key: float32 [4096, 1024], P('shard')
- update: bfloat16 [512, 32, 512], P('shard')
Inputs may be any that keep to these rules, and one draw needn't show every extreme that they name: `block_slot`: the entries are distinct; slot v is slot v % 4 of shard index v // 4; no shard index holds more than 4 blocks, and some shard index holds exactly 4.
All inputs are finite; a program needn't handle non-finite values.
Results may differ from a plain program's by a relative error of at most 0.006.
Values may be sent and summed in bfloat16 or wider, within the bound.
A program may use at most 128 MiB of HBM per device.

v0:
```python
import functools

import jax
import jax.numpy as jnp
from jax import lax
from jax.experimental import pallas as pl
from jax.experimental.pallas import tpu as pltpu
from jax.sharding import PartitionSpec as P

MESH = pl.DeviceIdType.MESH
GROUP = 4
PIECES = 2


def column_term(features, cotangent):
    return lax.dot_general(
        features, cotangent, (((0,), (0,)), ((), ())), preferred_element_type=jnp.float32
    )


def precondition(left_block, grad_block, right_block):
    left_part = jnp.einsum(
        "sij,sjk->sik", left_block, grad_block, preferred_element_type=jnp.float32
    ).astype(jnp.bfloat16)
    return jnp.einsum(
        "sij,sjk->isk", left_part, right_block, preferred_element_type=jnp.float32
    ).astype(jnp.bfloat16)


def plain_shards(tokens_x, key_grad, left_root, slot_grads, right_root, block_slot):
    n_shard = lax.axis_size("shard")
    n_rep = lax.axis_size("rep")
    own_rows = lax.psum_scatter(
        column_term(tokens_x, key_grad), "shard", scatter_dimension=0, tiled=True
    )
    grad_key = lax.psum(own_rows, "rep")
    slot_count = left_root.shape[0]
    half_slots = slot_count // n_rep
    first_slot = lax.axis_index("rep") * half_slots

    def own_half(values):
        return lax.dynamic_slice_in_dim(values, first_slot, half_slots, 0)

    product = precondition(own_half(left_root), own_half(slot_grads), own_half(right_root))
    received = lax.all_to_all(product, "shard", split_axis=0, concat_axis=1, tiled=True)
    joined = lax.all_gather(received, "rep", axis=1, tiled=True)
    owner = block_slot // slot_count
    within = block_slot % slot_count
    position = (
        within // half_slots * (n_shard * half_slots) + owner * half_slots + within % half_slots
    )
    update = jnp.take(joined, position, axis=1)
    return (grad_key, update)


def remote(src, dst, send_sem, recv_sem, axis, index):
    return pltpu.make_async_remote_copy(
        src_ref=src,
        dst_ref=dst,
        send_sem=send_sem,
        recv_sem=recv_sem,
        device_id={axis: index},
        device_id_type=MESH,
    )


def far_first(outer):
    return sorted(range(1, outer), key=lambda off: -min(off, outer - off)) + [0]


def kernel(
    n, slot_ref, x_ref, g_ref, lr_ref, sg_ref, rr_ref, og_ref, ou_ref,
    x_all, g_all, lr, sg, rr, prod, upd, mine, theirs, part, met, kept, passed, landed, half_out, half_in,
    local_sem, x_local, barrier_free, g_send, g_recv, x_send, x_recv, u_send, u_recv,
    a_send, a_recv, z_send, z_recv, r_send, r_recv, v_send, v_recv,
):
    me = lax.axis_index("shard")
    rep = lax.axis_index("rep")
    other_rep = 1 - rep
    q = me % GROUP
    z = me // GROUP
    base = z * GROUP
    outer = n // GROUP
    q_core = q + 1 - 2 * (q % 2)
    q_far = (q + 2) % GROUP
    q_both = (q_core + 2) % GROUP
    tok = x_ref.shape[0]
    cols = x_ref.shape[1] // n
    slots = lr_ref.shape[0]
    blocks = slot_ref.shape[0]
    offsets = far_first(outer)

    def tokens_of(index):
        return pl.ds(index * tok, tok)

    def columns(d, index):
        return pl.ds(pl.multiple_of((d * GROUP + index) * cols, 128), cols)

    copy_lr = pltpu.make_async_copy(lr_ref.at[:, :, rep], lr, local_sem.at[0])
    copy_sg = pltpu.make_async_copy(sg_ref, sg, local_sem.at[1])
    copy_rr = pltpu.make_async_copy(rr_ref, rr, local_sem.at[2])
    copy_g = pltpu.make_async_copy(g_ref, g_all.at[tokens_of(q)], local_sem.at[3])
    copies_x = []
    for d in range(outer):
        copies_x.append(
            pltpu.make_async_copy(
                x_ref.at[:, columns(d, q)], x_all.at[d, tokens_of(q)], x_local.at[d]
            )
        )
    copy_lr.start()
    copy_sg.start()
    copy_rr.start()
    copy_g.start()
    for copy in copies_x:
        copy.start()

    barrier = pltpu.get_barrier_semaphore()
    for step in range(1, n):
        pl.semaphore_signal(
            barrier, inc=1, device_id={"shard": (me + step) % n}, device_id_type=MESH
        )
    pl.semaphore_signal(barrier, inc=1, device_id={"rep": other_rep}, device_id_type=MESH)
    pl.semaphore_wait(barrier, n)

    sent = []

    def send(*args):
        copy = remote(*args)
        copy.start()
        sent.append(copy)

    for order, target in enumerate((q_far, q_core)):
        send(
            g_ref, g_all.at[tokens_of(q)], g_send.at[order], g_recv.at[q], "shard", base + target
        )
    for order, off in enumerate(offsets):
        d = (z + off) % outer
        for place, target in enumerate((q_far, q_both, q_core)):
            send(
                x_ref.at[:, columns(d, target)],
                x_all.at[d, tokens_of(q)],
                x_send.at[order, place],
                x_recv.at[q, d],
                "shard",
                base + target,
            )

    copy_lr.wait()
    copy_sg.wait()
    copy_rr.wait()
    height = lr.shape[2]
    width = lr.shape[3]
    for s in range(slots):
        left = jnp.dot(
            lr[s].reshape(n * height, width), sg[s], preferred_element_type=jnp.float32
        ).astype(jnp.bfloat16)
        both = jnp.dot(left, rr[s], preferred_element_type=jnp.float32).astype(jnp.bfloat16)
        prod[:, s] = both.reshape(n, height, width)
    for step in range(1, n):
        target = (me + step) % n
        send(
            prod.at[target],
            upd.at[pl.ds(me * slots, slots)],
            u_send.at[step],
            u_recv.at[me],
            "shard",
            target,
        )
    upd[pl.ds(me * slots, slots)] = prod[me]

    def arrive(dst, recv_sem):
        remote(dst, dst, barrier_free, recv_sem, "shard", (me + 1) % n).wait_recv()

    arrive(g_all.at[tokens_of(q_far)], g_recv.at[q_far])
    send(
        g_all.at[tokens_of(q_far)],
        g_all.at[tokens_of(q_far)],
        g_send.at[2],
        g_recv.at[q_far],
        "shard",
        base + q_core,
    )
    copy_g.wait()
    arrive(g_all.at[tokens_of(q_core)], g_recv.at[q_core])
    arrive(g_all.at[tokens_of(q_both)], g_recv.at[q_both])
    for copy in copies_x:
        copy.wait()

    piece = kept.shape[3]
    half = PIECES * piece

    def partial(d, side):
        start = pl.multiple_of(side * half, 128)
        return lax.dot_general(
            x_all[d],
            g_all[:, pl.ds(start, half)],
            (((0,), (0,)), ((), ())),
            preferred_element_type=jnp.float32,
        )

    def place_of(side, p):
        return pl.ds(pl.multiple_of(side * half + p * piece, 128), piece)

    def pass_on(order):
        off = offsets[order]
        for p in range(PIECES):
            arrive(met.at[order, p], a_recv.at[order, p])
            total = kept[order, p] + met[order, p].astype(jnp.float32)
            if off == 0:
                kept[order, p] = total
            else:
                passed[order, p] = total.astype(jnp.bfloat16)
                send(
                    passed.at[order, p],
                    landed.at[z, p],
                    z_send.at[order, p],
                    z_recv.at[z, p],
                    "shard",
                    (z + off) % outer * GROUP + q,
                )

    for order, off in enumerate(offsets):
        d = (z + off) % outer
        for source in (q_core, q_far, q_both):
            arrive(x_all.at[d, tokens_of(source)], x_recv.at[source, d])
        value = partial(d, other_rep)
        for p in range(PIECES):
            part[order, p] = value[:, p * piece : (p + 1) * piece].astype(jnp.bfloat16)
            send(
                part.at[order, p],
                met.at[order, p],
                a_send.at[order, p],
                a_recv.at[order, p],
                "rep",
                other_rep,
            )
        value = partial(d, rep)
        for p in range(PIECES):
            kept[order, p] = value[:, p * piece : (p + 1) * piece]
        if order > 0:
            pass_on(order - 1)
    pass_on(outer - 1)

    for step in range(1, n):
        source = (me + n - step) % n
        arrive(upd.at[pl.ds(source * slots, slots)], u_recv.at[source])

    def pick(b, carry):
        mine[b] = upd[slot_ref[b]]
        return carry

    lax.fori_loop(0, blocks, pick, 0)
    send(mine, theirs, v_send, v_recv, "rep", other_rep)
    ou_ref[rep] = mine[...]

    for p in range(PIECES):
        total = kept[outer - 1, p]
        for off in offsets[:-1]:
            source = (z + outer - off) % outer
            arrive(landed.at[source, p], z_recv.at[source, p])
            total = total + landed[source, p].astype(jnp.float32)
        half_out[p] = total.astype(jnp.bfloat16)
        send(half_out.at[p], half_in.at[p], r_send.at[p], r_recv.at[p], "rep", other_rep)

    for p in range(PIECES):
        og_ref[:, place_of(rep, p)] = half_out[p]
    arrive(theirs, v_recv)
    ou_ref[other_rep] = theirs[...]
    for p in range(PIECES):
        arrive(half_in.at[p], r_recv.at[p])
        og_ref[:, place_of(other_rep, p)] = half_in[p]
    for copy in sent:
        copy.wait_send()


def fused_shards(tokens_x, key_grad, left_root, slot_grads, right_root, block_slot):
    n = lax.axis_size("shard")
    n_rep = lax.axis_size("rep")
    outer = n // GROUP
    tok, d_model = tokens_x.shape
    key_width = key_grad.shape[1]
    cols = d_model // n
    slots, order_b, width = left_root.shape
    height = order_b // n // n_rep
    blocks = block_slot.shape[0]
    piece = key_width // n_rep // PIECES
    bf16, f32 = jnp.bfloat16, jnp.float32
    dma = pltpu.SemaphoreType.DMA
    any_spec = pl.BlockSpec(memory_space=pl.ANY)
    vmem_spec = pl.BlockSpec(memory_space=pltpu.VMEM)
    sums, rows = pl.pallas_call(
        functools.partial(kernel, n),
        out_shape=(
            jax.ShapeDtypeStruct((cols, key_width), bf16),
            jax.ShapeDtypeStruct((n_rep, blocks, height, width), bf16),
        ),
        in_specs=[pl.BlockSpec(memory_space=pltpu.SMEM)] + [any_spec] * 5,
        out_specs=(vmem_spec, vmem_spec),
        scratch_shapes=[
            pltpu.VMEM((outer, GROUP * tok, cols), bf16),
            pltpu.VMEM((GROUP * tok, key_width), bf16),
            pltpu.VMEM((slots, n, height, width), bf16),
            pltpu.VMEM(slot_grads.shape, bf16),
            pltpu.VMEM(right_root.shape, bf16),
            pltpu.VMEM((n, slots, height, width), bf16),
            pltpu.VMEM((n * slots, height, width), bf16),
            pltpu.VMEM((blocks, height, width), bf16),
            pltpu.VMEM((blocks, height, width), bf16),
            pltpu.VMEM((outer, PIECES, cols, piece), bf16),
            pltpu.VMEM((outer, PIECES, cols, piece), bf16),
            pltpu.VMEM((outer, PIECES, cols, piece), f32),
            pltpu.VMEM((outer - 1, PIECES, cols, piece), bf16),
            pltpu.VMEM((outer, PIECES, cols, piece), bf16),
            pltpu.VMEM((PIECES, cols, piece), bf16),
            pltpu.VMEM((PIECES, cols, piece), bf16),
            dma((4,)),
            dma((outer,)),
            dma,
            dma((3,)),
            dma((GROUP,)),
            dma((outer, 3)),
            dma((GROUP, outer)),
            dma((n,)),
            dma((n,)),
            dma((outer, PIECES)),
            dma((outer, PIECES)),
            dma((outer - 1, PIECES)),
            dma((outer, PIECES)),
            dma((PIECES,)),
            dma((PIECES,)),
            dma,
            dma,
        ],
        compiler_params=pltpu.CompilerParams(
            collective_id=0, has_side_effects=True, vmem_limit_bytes=60 * 1024 * 1024
        ),
    )(
        block_slot,
        tokens_x,
        key_grad,
        left_root.reshape(slots, n, n_rep, height, width),
        slot_grads,
        right_root,
    )
    grad_key = sums.astype(f32)
    update = jnp.transpose(rows, (0, 2, 1, 3)).reshape(n_rep * height, blocks, width)
    return (grad_key, update)


def shards(tokens_x, key_grad, left_root, slot_grads, right_root, block_slot):
    n = lax.axis_size("shard")
    n_rep = lax.axis_size("rep")
    aligned = (
        n_rep == 2
        and n % GROUP == 0
        and n > GROUP
        and tokens_x.shape[1] % (n * 128) == 0
        and key_grad.shape[1] % (n_rep * PIECES * 128) == 0
        and tokens_x.shape[0] % 16 == 0
        and left_root.shape[1] % (n * n_rep * 16) == 0
        and left_root.shape[2] % 128 == 0
    )
    program = fused_shards if aligned else plain_shards
    return program(tokens_x, key_grad, left_root, slot_grads, right_root, block_slot)


def solution(mesh):
    return jax.shard_map(
        shards,
        mesh=mesh,
        in_specs=(
            P(("rep", "shard"), None),
            P(("rep", "shard"), None),
            P("shard", None, None),
            P("shard", None, None),
            P("shard", None, None),
            P(),
        ),
        out_specs=(P("shard", None), P("shard", None, None)),
        check_vma=False,
    )
```

profile of v0, /device:TPU:0, one launch (start us, length us, event | category | flops | bytes accessed | tf_op | source)
XLA Modules:
  0.0 84.7 jit_solution(18036290338881226330)
XLA Ops:
  0.6 80.2 %shard_map.77 = (bf16[256,1024]{1,0:T(8,128)(2,1)}, bf16[2,32,16,512]{3,2,1,0:T(8,128)(2,1)}) custom-call(s32[32]{0:T(128)} %slot_ref.1, bf16[256,4096]{1,0:T(8,128)(2,1)} %x_ref.1, bf16[256,1024]{1,0:T(8,128)(2,1)} %g_ref.1, bf16[4,16,2,16,512]{4,3,2,1,0:T(8,128)(2,1)} %bitcast.3, bf16[4,512,512]{2,1,0:T(8,128)(2,1)} %sg_ref.1, bf16[4,512,512]{2,1,0:T(8,128)(2,1)} %rr_ref.1), custom_call_target="tpu_custom_call" | custom-call | tf_op jit(solution)/shard_map/pallas_call | solution.py:291
  80.8 0.0 copy-start
  80.8 2.8 %copy.8 = bf16[2,16,32,512]{3,2,1,0:T(8,128)(2,1)} copy(bf16[2,16,32,512]{3,1,2,0:T(8,128)(2,1)} %bitcast.5) | data formatting | bytes 2097152 | tf_op jit(solution)/shard_map/transpose | solution.py:346
  83.6 0.0 copy-done
  83.6 1.1 %convert_element_type.3 = f32[256,1024]{1,0:T(8,128)} convert(bf16[256,1024]{1,0:T(8,128)(2,1)S(1)} %copy-done) | non-fusion elementwise | flops 262144 | bytes 1572864 | tf_op jit(solution)/shard_map/convert_element_type | solution.py:345
Async XLA Ops:
  80.8 2.8 %copy-start = (bf16[256,1024]{1,0:T(8,128)(2,1)S(1)}, bf16[256,1024]{1,0:T(8,128)(2,1)}, u32[]{:S(2)}) copy-start(bf16[256,1024]{1,0:T(8,128)(2,1)} %get-tuple-element.4) | copy-start | bytes 1572868
where the time goes:
time: 84.9 us; the launch traced here: 84.7 us
  Pallas kernels  80.2 us (94%)
  local copies, waits for them, and re-layouts  2.84 us (3%)
  other arithmetic  1.09 us (1%)
    pallas_call x1, Pallas kernels, fused_shards(): pl.pallas_call(functools.partial(kernel, n), out_shape=(jax.ShapeDtypeStr...  80.2 us
    transpose x1, local copies, waits for them, and re-layouts, fused_shards(): jnp.transpose(rows, (0, 2, 1, 3)).reshape(n_rep * height, blocks, width)  2.83 us

commit v1 on v0

v1 whole, which is shorter than its diff:
```python
import jax
import jax.numpy as jnp
from jax import lax
from jax.experimental import pallas as pl
from jax.experimental.pallas import tpu as pltpu
from jax.sharding import PartitionSpec as P

MESH = pl.DeviceIdType.MESH
GROUP = 4
PARTS = 2
PIECES = 2


def column_term(features, cotangent):
    return lax.dot_general(
        features, cotangent, (((0,), (0,)), ((), ())), preferred_element_type=jnp.float32
    )


def precondition(left_block, grad_block, right_block):
    left_part = jnp.einsum(
        "sij,sjk->sik", left_block, grad_block, preferred_element_type=jnp.float32
    ).astype(jnp.bfloat16)
    return jnp.einsum(
        "sij,sjk->isk", left_part, right_block, preferred_element_type=jnp.float32
    ).astype(jnp.bfloat16)


def plain_shards(tokens_x, key_grad, left_root, slot_grads, right_root, block_slot):
    n_shard = lax.axis_size("shard")
    n_rep = lax.axis_size("rep")
    own_rows = lax.psum_scatter(
        column_term(tokens_x, key_grad), "shard", scatter_dimension=0, tiled=True
    )
    grad_key = lax.psum(own_rows, "rep")
    slot_count = left_root.shape[0]
    half_slots = slot_count // n_rep
    first_slot = lax.axis_index("rep") * half_slots

    def own_half(values):
        return lax.dynamic_slice_in_dim(values, first_slot, half_slots, 0)

    product = precondition(own_half(left_root), own_half(slot_grads), own_half(right_root))
    received = lax.all_to_all(product, "shard", split_axis=0, concat_axis=1, tiled=True)
    joined = lax.all_gather(received, "rep", axis=1, tiled=True)
    owner = block_slot // slot_count
    within = block_slot % slot_count
    position = (
        within // half_slots * (n_shard * half_slots) + owner * half_slots + within % half_slots
    )
    update = jnp.take(joined, position, axis=1)
    return (grad_key, update)


def remote(src, dst, send_sem, recv_sem, target):
    return pltpu.make_async_remote_copy(
        src_ref=src,
        dst_ref=dst,
        send_sem=send_sem,
        recv_sem=recv_sem,
        device_id=target,
        device_id_type=MESH,
    )


def kernel(
    slot_ref, x_ref, g_ref, lr_ref, sg_ref, rr_ref, og_ref, ou_ref,
    x_all, g_all, lr, sg, rr, prod, relay, upd, hot, part, met, kept, passed, first, second,
    sums, rows,
    load_sem, x_load, out_sem, send_sem, g_recv, x_recv, u_recv, y_recv, a_recv, s_recv, t_recv,
    r_recv, v_recv,
):
    me = lax.axis_index("shard")
    rep = lax.axis_index("rep")
    other_rep = 1 - rep
    q = me % GROUP
    z = me // GROUP
    base = z * GROUP
    core = q + 1 - 2 * (q % 2)
    far = (q + 2) % GROUP
    both = (core + 2) % GROUP
    relatives = (q, core, far, both)
    z_near = z + 1 - 2 * (z % 2)
    z_half = (z + 2) % 4
    z_last = 3 - z
    order_of = (z_last, z_near, z_half, z)
    tok = g_ref.shape[0]
    unit = met.shape[1]
    half = met.shape[2]
    slots = lr.shape[0]
    n = lr.shape[1]
    height = lr.shape[2]
    width = lr.shape[3]
    blocks = slot_ref.shape[0]
    piece = width // PIECES

    def shard(index):
        return {"shard": index}

    across = {"rep": other_rep}
    near = shard(z_near * GROUP + q)
    opposite = shard(z_half * GROUP + q)

    def tokens_of(index):
        return pl.ds(index * tok, tok)

    def keys_of(side):
        return pl.ds(pl.multiple_of(side * half, 128), half)

    def columns(o, index, r):
        start = (order_of[o] * GROUP + index) * (PARTS * unit) + r * unit
        return pl.ds(pl.multiple_of(start, 128), unit)

    def unit_of(r):
        return pl.ds(r * unit, unit)

    copy_lr = pltpu.make_async_copy(lr_ref.at[:, :, rep], lr, load_sem.at[0])
    copy_sg = pltpu.make_async_copy(sg_ref, sg, load_sem.at[1])
    copy_rr = pltpu.make_async_copy(rr_ref, rr, load_sem.at[2])
    copy_g = pltpu.make_async_copy(g_ref, g_all.at[tokens_of(q)], load_sem.at[3])
    copies_x = []
    for o in range(4):
        start = pl.multiple_of((order_of[o] * GROUP + q) * (PARTS * unit), 128)
        copies_x.append(
            pltpu.make_async_copy(
                x_ref.at[:, pl.ds(start, PARTS * unit)], x_all.at[o, tokens_of(q)], x_load.at[o]
            )
        )

    barrier = pltpu.get_barrier_semaphore()
    peers = [across]
    for index in (core, far, both):
        peers.append(shard(base + index))
    for level in (z_near, z_half, z_last):
        peers.append(shard(level * GROUP + q))
    for peer in peers:
        pl.semaphore_signal(barrier, inc=1, device_id=peer, device_id_type=MESH)
    copy_lr.start()
    copy_sg.start()
    copy_rr.start()
    copy_g.start()
    for copy in copies_x:
        copy.start()
    pl.semaphore_wait(barrier, len(peers))

    def send(src, dst, kind, recv_sem, target):
        remote(src, dst, send_sem.at[kind], recv_sem, target).start()

    def arrive(ref, recv_sem):
        remote(ref, ref, send_sem.at[0], recv_sem, across).wait_recv()

    def send_g(which, target, place):
        keys = keys_of(other_rep if which == 0 else rep)
        send(
            g_ref.at[:, keys], g_all.at[tokens_of(q), keys], 0, g_recv.at[which, place],
            shard(base + target),
        )

    def send_x(o, r):
        for target in (far, both, core):
            send(
                x_ref.at[:, columns(o, target, r)],
                x_all.at[o, tokens_of(q), unit_of(r)],
                1,
                x_recv.at[o, r],
                shard(base + target),
            )

    send_g(0, far, 0)
    send_g(0, core, 1)
    for r in range(PARTS):
        send_x(0, r)
    for r in range(PARTS):
        send_x(1, r)
    send_g(1, far, 0)
    send_g(1, core, 1)
    for o in (2, 3):
        for r in range(PARTS):
            send_x(o, r)

    chosen = jnp.zeros((blocks, 128), jnp.int32)
    row = lax.broadcasted_iota(jnp.int32, (blocks, 128), 0)
    for b in range(blocks):
        chosen = jnp.where(row == b, slot_ref[b], chosen)
    lane = lax.broadcasted_iota(jnp.int32, (blocks, 128), 1)
    per = 4 * slots * height
    for k, index in enumerate(relatives):
        for part_of in range(per // 128):
            place = lane + part_of * 128
            source = place // (slots * height) * (GROUP * slots) + index * slots
            source = source + place // height % slots
            same = source == chosen
            for i in range(height):
                hit = jnp.logical_and(same, place % height == i)
                hot[k, pl.ds(i * blocks, blocks), pl.ds(part_of * 128, 128)] = jnp.where(
                    hit, 1.0, 0.0
                ).astype(jnp.bfloat16)

    copy_lr.wait()
    copy_sg.wait()
    copy_rr.wait()
    for s in range(slots):
        left = jnp.dot(
            lr[s].reshape(n * height, width), sg[s], preferred_element_type=jnp.float32
        ).astype(jnp.bfloat16)
        full = jnp.dot(left, rr[s], preferred_element_type=jnp.float32).astype(jnp.bfloat16)
        prod[:, s] = full.reshape(4, GROUP, height, width)
    for level in (z_half, z_last, z_near):
        send(prod.at[level], relay.at[z], 2, u_recv.at[0], shard(level * GROUP + q))
    relay[z] = prod[z]

    def gather_g(which):
        keys = keys_of(other_rep if which == 0 else rep)
        view = g_all.at[tokens_of(far), keys]
        arrive(view, g_recv.at[which, 0])
        send(view, view, 0, g_recv.at[which, 2], shard(base + core))
        arrive(g_all.at[tokens_of(core), keys], g_recv.at[which, 1])
        arrive(g_all.at[tokens_of(both), keys], g_recv.at[which, 2])

    def partial(o, r, side):
        return lax.dot_general(
            x_all[o, :, r * unit : (r + 1) * unit],
            g_all[:, keys_of(side)],
            (((0,), (0,)), ((), ())),
            preferred_element_type=jnp.float32,
        )

    def give(o, r):
        if r == 0:
            copies_x[o].wait()
        arrive(x_all.at[o, pl.ds(0, 3 * tok), unit_of(r)], x_recv.at[o, r])
        part[o * PARTS + r] = partial(o, r, other_rep).astype(jnp.bfloat16)
        send(
            part.at[o * PARTS + r], met.at[o * PARTS + r], 3, a_recv.at[o * PARTS + r], across
        )

    def keep(o, r):
        kept[o * PARTS + r] = partial(o, r, rep)

    def total_of(o, r):
        u = o * PARTS + r
        arrive(met.at[u], a_recv.at[u])
        return kept[u] + met[u].astype(jnp.float32)

    def pass_near(o, r):
        u = o * PARTS + r
        passed[u] = total_of(o, r).astype(jnp.bfloat16)
        send(passed.at[u], first.at[u], 4, s_recv.at[u], near)

    def pass_half(r):
        u = 2 * PARTS + r
        total = total_of(2, r)
        arrive(first.at[r], s_recv.at[r])
        passed[u] = (total + first[r].astype(jnp.float32)).astype(jnp.bfloat16)
        send(passed.at[u], second.at[r], 5, t_recv.at[r], opposite)

    def finish(r):
        total = total_of(3, r)
        arrive(first.at[PARTS + r], s_recv.at[PARTS + r])
        total = total + first[PARTS + r].astype(jnp.float32)
        arrive(second.at[r], t_recv.at[r])
        total = total + second[r].astype(jnp.float32)
        view = sums.at[rep, unit_of(r)]
        sums[rep, unit_of(r)] = total.astype(jnp.bfloat16)
        send(view, view, 6, r_recv.at[r], across)

    def slice_of(p):
        return pl.ds(p * piece, piece)

    def spread():
        arrive(relay.at[pl.ds(0, 3)], u_recv.at[0])
        for p in range(PIECES):
            for k, target in ((2, far), (3, both), (1, core)):
                send(
                    relay.at[:, :, target, :, slice_of(p)],
                    upd.at[k, :, :, :, slice_of(p)],
                    7,
                    y_recv.at[p],
                    shard(base + target),
                )

    def select(p):
        cols = slice(p * piece, (p + 1) * piece)
        arrive(upd.at[pl.ds(1, 3), :, :, :, slice_of(p)], y_recv.at[p])
        value = jnp.dot(
            hot[0], relay[:, :, q, :, cols].reshape(per, piece), preferred_element_type=jnp.float32
        )
        for k in range(1, 4):
            value = value + jnp.dot(
                hot[k], upd[k, :, :, :, cols].reshape(per, piece),
                preferred_element_type=jnp.float32,
            )
        rows[rep, :, :, cols] = value.astype(jnp.bfloat16).reshape(height, blocks, piece)
        view = rows.at[rep, :, :, slice_of(p)]
        send(view, view, 8, v_recv.at[p], across)

    copy_g.wait()
    gather_g(0)
    for o in (0, 1):
        for r in range(PARTS):
            give(o, r)
    gather_g(1)
    for o in (0, 1):
        for r in range(PARTS):
            keep(o, r)
            pass_near(o, r)
    give(2, 0)
    keep(2, 0)
    give(2, 1)
    keep(2, 1)
    spread()
    give(3, 0)
    keep(3, 0)
    pass_half(0)
    give(3, 1)
    keep(3, 1)
    pass_half(1)
    for r in range(PARTS):
        finish(r)
    for p in range(PIECES):
        select(p)

    outs = []

    def put(src, dst):
        copy = pltpu.make_async_copy(src, dst, out_sem.at[len(outs)])
        copy.start()
        outs.append(copy)

    put(sums.at[rep], og_ref.at[:, keys_of(rep)])
    put(rows.at[rep], ou_ref.at[rep])
    for r in range(PARTS):
        view = sums.at[other_rep, unit_of(r)]
        arrive(view, r_recv.at[r])
        put(view, og_ref.at[unit_of(r), keys_of(other_rep)])
    for p in range(PIECES):
        view = rows.at[other_rep, :, :, slice_of(p)]
        arrive(view, v_recv.at[p])
        put(view, ou_ref.at[other_rep, :, :, slice_of(p)])

    def drain(ref, kind):
        remote(ref, ref, send_sem.at[kind], send_sem.at[kind], across).wait_send()

    drain(x_all.at[pl.ds(0, 3)], 0)
    drain(x_all.at[pl.ds(0, 3)], 1)
    drain(relay.at[pl.ds(0, 3)], 2)
    drain(met, 3)
    drain(met.at[pl.ds(0, 2 * PARTS)], 4)
    drain(met.at[pl.ds(0, PARTS)], 5)
    drain(met.at[pl.ds(0, PARTS)], 6)
    drain(relay.at[pl.ds(0, 3)], 7)
    drain(rows.at[0], 8)
    for copy in outs:
        copy.wait()


def fused_shards(tokens_x, key_grad, left_root, slot_grads, right_root, block_slot):
    n = lax.axis_size("shard")
    n_rep = lax.axis_size("rep")
    tok, d_model = tokens_x.shape
    key_width = key_grad.shape[1]
    cols = d_model // n
    slots, order_b, width = left_root.shape
    height = order_b // n // n_rep
    blocks = block_slot.shape[0]
    half = key_width // n_rep
    unit = cols // PARTS
    per = 4 * slots * height
    bf16, f32 = jnp.bfloat16, jnp.float32
    dma = pltpu.SemaphoreType.DMA
    any_spec = pl.BlockSpec(memory_space=pl.ANY)
    sums, rows = pl.pallas_call(
        kernel,
        out_shape=(
            jax.ShapeDtypeStruct((cols, key_width), bf16),
            jax.ShapeDtypeStruct((n_rep, height, blocks, width), bf16),
        ),
        in_specs=[pl.BlockSpec(memory_space=pltpu.SMEM)] + [any_spec] * 5,
        out_specs=(any_spec, any_spec),
        scratch_shapes=[
            pltpu.VMEM((4, GROUP * tok, cols), bf16),
            pltpu.VMEM((GROUP * tok, key_width), bf16),
            pltpu.VMEM((slots, n, height, width), bf16),
            pltpu.VMEM(slot_grads.shape, bf16),
            pltpu.VMEM(right_root.shape, bf16),
            pltpu.VMEM((4, slots, GROUP, height, width), bf16),
            pltpu.VMEM((4, slots, GROUP, height, width), bf16),
            pltpu.VMEM((4, 4, slots, height, width), bf16),
            pltpu.VMEM((4, height * blocks, per), bf16),
            pltpu.VMEM((4 * PARTS, unit, half), bf16),
            pltpu.VMEM((4 * PARTS, unit, half), bf16),
            pltpu.VMEM((4 * PARTS, unit, half), f32),
            pltpu.VMEM((3 * PARTS, unit, half), bf16),
            pltpu.VMEM((2 * PARTS, unit, half), bf16),
            pltpu.VMEM((PARTS, unit, half), bf16),
            pltpu.VMEM((n_rep, cols, half), bf16),
            pltpu.VMEM((n_rep, height, blocks, width), bf16),
            dma((4,)),
            dma((4,)),
            dma((2 + PARTS + PIECES,)),
            dma((9,)),
            dma((2, 3)),
            dma((4, PARTS)),
            dma((1,)),
            dma((PIECES,)),
            dma((4 * PARTS,)),
            dma((2 * PARTS,)),
            dma((PARTS,)),
            dma((PARTS,)),
            dma((PIECES,)),
        ],
        compiler_params=pltpu.CompilerParams(
            collective_id=0, has_side_effects=True, vmem_limit_bytes=60 * 1024 * 1024
        ),
    )(
        block_slot,
        tokens_x,
        key_grad,
        left_root.reshape(slots, n, n_rep, height, width),
        slot_grads,
        right_root,
    )
    return (sums.astype(f32), rows.reshape(n_rep * height, blocks, width))


def shards(tokens_x, key_grad, left_root, slot_grads, right_root, block_slot):
    n = lax.axis_size("shard")
    n_rep = lax.axis_size("rep")
    cols = tokens_x.shape[1] // n
    width = left_root.shape[2]
    per = left_root.shape[0] * left_root.shape[1] // (GROUP * n_rep)
    aligned = (
        n_rep == 2
        and n == 4 * GROUP
        and tokens_x.shape[1] % (n * PARTS * 128) == 0
        and key_grad.shape[1] % (n_rep * 128) == 0
        and 2 * key_grad.shape[1] == GROUP * PARTS * cols
        and tokens_x.shape[0] % 16 == 0
        and left_root.shape[1] % (n * n_rep * 16) == 0
        and width % (PIECES * 128) == 0
        and per % 128 == 0
        and block_slot.shape[0] % 16 == 0
    )
    program = fused_shards if aligned else plain_shards
    return program(tokens_x, key_grad, left_root, slot_grads, right_root, block_slot)


def solution(mesh):
    return jax.shard_map(
        shards,
        mesh=mesh,
        in_specs=(
            P(("rep", "shard"), None),
            P(("rep", "shard"), None),
            P("shard", None, None),
            P("shard", None, None),
            P("shard", None, None),
            P(),
        ),
        out_specs=(P("shard", None), P("shard", None, None)),
        check_vma=False,
    )
```

time: 84.9 us -> 74.2 us (0.87)
  Pallas kernels: 80.2 us -> 70.2 us
  local copies, waits for them, and re-layouts: 2.84 us -> 0.97 us
  other arithmetic: 1.09 us -> 2.21 us
    pallas_call x1, Pallas kernels: 80.2 us -> 70.2 us  [fused_shards(): pl.pallas_call(kernel, out_shape=(jax.ShapeDtypeStruct((cols, key_width),...]
    transpose x1 -> x0, local copies, waits for them, and re-layouts: 2.83 us -> none  [fused_shards(): jnp.transpose(rows, (0, 2, 1, 3)).reshape(n_rep * height, blocks, width)]
    convert_element_type x1, other arithmetic: 1.09 us -> 2.21 us  [fused_shards(): return (sums.astype(f32), rows.reshape(n_rep * height, blocks, width))]
    unnamed x2 -> x3, local copies, waits for them, and re-layouts: 0.01 us -> 0.97 us
where the time goes in v1:
time: 74.2 us; the launch traced here: 74 us
  Pallas kernels  70.2 us (95%)
  other arithmetic  2.21 us (3%)
  local copies, waits for them, and re-layouts  0.97 us (1%)
    pallas_call x1, Pallas kernels, fused_shards(): pl.pallas_call(kernel, out_shape=(jax.ShapeDtypeStruct((cols, key_width),...  70.2 us
    convert_element_type x1, other arithmetic, fused_shards(): return (sums.astype(f32), rows.reshape(n_rep * height, blocks, width))  2.21 us

profile of v1, /device:TPU:0, one launch (start us, length us, event | category | flops | bytes accessed | tf_op | source)
XLA Modules:
  0.0 74.0 jit_solution(7692748640130421444)
XLA Ops:
  0.6 70.2 %shard_map.77 = (bf16[256,1024]{1,0:T(8,128)(2,1)}, bf16[2,16,32,512]{3,2,1,0:T(8,128)(2,1)}) custom-call(s32[32]{0:T(128)} %slot_ref.1, bf16[256,4096]{1,0:T(8,128)(2,1)} %x_ref.1, bf16[256,1024]{1,0:T(8,128)(2,1)} %g_ref.1, bf16[4,16,2,16,512]{4,3,2,1,0:T(8,128)(2,1)} %bitcast.2, bf16[4,512,512]{2,1,0:T(8,128)(2,1)} %sg_ref.1, bf16[4,512,512]{2,1,0:T(8,128)(2,1)} %rr_ref.1), custom_call_target="tpu_custom_call" | custom-call | tf_op jit(solution)/shard_map/pallas_call | solution.py:372
  70.8 0.0 copy-start
  70.8 2.2 %convert_element_type.3 = f32[256,1024]{1,0:T(8,128)} convert(bf16[256,1024]{1,0:T(8,128)(2,1)} %get-tuple-element.4) | non-fusion elementwise | flops 262144 | bytes 1572864 | tf_op jit(solution)/shard_map/convert_element_type | solution.py:423
  73.0 0.0 copy-done
  73.0 1.0 %copy.9 = bf16[32,32,512]{2,1,0:T(8,128)(2,1)} copy(bf16[32,32,512]{2,1,0:T(8,128)(2,1)S(1)} %bitcast.3) | data formatting | bytes 2097152
Async XLA Ops:
  70.8 2.2 %copy-start = (bf16[2,16,32,512]{3,2,1,0:T(8,128)(2,1)S(1)}, bf16[2,16,32,512]{3,2,1,0:T(8,128)(2,1)}, u32[]{:S(2)}) copy-start(bf16[2,16,32,512]{3,2,1,0:T(8,128)(2,1)} %get-tuple-element.5) | copy-start | bytes 3145732

commit v2 on v1

--- a/solution.py
+++ b/solution.py
@@ -8,7 +8,7 @@
 MESH = pl.DeviceIdType.MESH
 GROUP = 4
 PARTS = 2
-PIECES = 2
+PIECES = 4
 
 
 def column_term(features, cotangent):
@@ -66,9 +66,10 @@
 def kernel(
     slot_ref, x_ref, g_ref, lr_ref, sg_ref, rr_ref, og_ref, ou_ref,
     x_all, g_all, lr, sg, rr, prod, relay, upd, hot, part, met, kept, passed, first, second,
-    sums, rows,
-    load_sem, x_load, out_sem, send_sem, g_recv, x_recv, u_recv, y_recv, a_recv, s_recv, t_recv,
-    r_recv, v_recv,
+    x_own, part_own, met_own, kept_own, turned, got,
+    sums, rows, wide,
+    open_sem, load_sem, x_load, out_sem, send_sem, g_recv, x_recv, u_recv, y_recv, a_recv, s_recv, t_recv,
+    r_recv, v_recv, d_load, d_recv, e_recv, f_recv,
 ):
     me = lax.axis_index("shard")
     rep = lax.axis_index("rep")
@@ -83,7 +84,7 @@
     z_near = z + 1 - 2 * (z % 2)
     z_half = (z + 2) % 4
     z_last = 3 - z
-    order_of = (z_last, z_near, z_half, z)
+    order_of = (z_last, z_half, z_near, z)
     tok = g_ref.shape[0]
     unit = met.shape[1]
     half = met.shape[2]
@@ -119,7 +120,7 @@
     copy_rr = pltpu.make_async_copy(rr_ref, rr, load_sem.at[2])
     copy_g = pltpu.make_async_copy(g_ref, g_all.at[tokens_of(q)], load_sem.at[3])
     copies_x = []
-    for o in range(4):
+    for o in range(3):
         start = pl.multiple_of((order_of[o] * GROUP + q) * (PARTS * unit), 128)
         copies_x.append(
             pltpu.make_async_copy(
@@ -127,21 +128,52 @@
             )
         )
 
+    lower = q - q % 2
+
+    def wide_columns(index):
+        start = (z * GROUP + index) * (PARTS * unit)
+        return pl.ds(pl.multiple_of(start, 128), PARTS * unit)
+
+    own_tokens = pl.ds((q % 2) * tok, tok)
+    copies_own = []
+    for w, index in enumerate((q, far)):
+        copies_own.append(
+            pltpu.make_async_copy(
+                x_ref.at[:, wide_columns(index)], x_own.at[w, own_tokens], d_load.at[w]
+            )
+        )
+
     barrier = pltpu.get_barrier_semaphore()
-    peers = [across]
+    peers = [across, near]
     for index in (core, far, both):
         peers.append(shard(base + index))
-    for level in (z_near, z_half, z_last):
-        peers.append(shard(level * GROUP + q))
+    inner = jnp.logical_and(z > 0, z < 3)
+    facing = shard(z_last * GROUP + q)
     for peer in peers:
         pl.semaphore_signal(barrier, inc=1, device_id=peer, device_id_type=MESH)
+
+    @pl.when(inner)
+    def _():
+        pl.semaphore_signal(barrier, inc=1, device_id=facing, device_id_type=MESH)
+
+    copy_g.start()
+    for copy in copies_own:
+        copy.start()
     copy_lr.start()
     copy_sg.start()
     copy_rr.start()
-    copy_g.start()
     for copy in copies_x:
         copy.start()
-    pl.semaphore_wait(barrier, len(peers))
+    copy_g.wait()
+    @pl.when(inner)
+    def _():
+        pl.semaphore_wait(barrier, len(peers) + 1)
+        pl.semaphore_signal(open_sem, inc=1, device_id=facing, device_id_type=MESH)
+
+    @pl.when(jnp.logical_not(inner))
+    def _():
+        pl.semaphore_wait(barrier, len(peers))
+
 
     def send(src, dst, kind, recv_sem, target):
         remote(src, dst, send_sem.at[kind], recv_sem, target).start()
@@ -151,10 +183,8 @@
 
     def send_g(which, target, place):
         keys = keys_of(other_rep if which == 0 else rep)
-        send(
-            g_ref.at[:, keys], g_all.at[tokens_of(q), keys], 0, g_recv.at[which, place],
-            shard(base + target),
-        )
+        view = g_all.at[tokens_of(q), keys]
+        send(view, view, 0, g_recv.at[which, place], shard(base + target))
 
     def send_x(o, r):
         for target in (far, both, core):
@@ -168,15 +198,62 @@
 
     send_g(0, far, 0)
     send_g(0, core, 1)
+    for w, index in enumerate((core, both)):
+        send(
+            x_ref.at[:, wide_columns(index)], x_own.at[w, own_tokens], 9, d_recv.at[w],
+            shard(base + core),
+        )
+    send_g(1, core, 1)
     for r in range(PARTS):
         send_x(0, r)
-    for r in range(PARTS):
-        send_x(1, r)
     send_g(1, far, 0)
-    send_g(1, core, 1)
-    for o in (2, 3):
+    for o in (1, 2):
         for r in range(PARTS):
             send_x(o, r)
+
+    pair = pl.ds(lower * tok, 2 * tok)
+    mate_tokens = pl.ds((1 - q % 2) * tok, tok)
+
+    def partial_own(w, r, side):
+        return lax.dot_general(
+            x_own[w, :, r * unit : (r + 1) * unit],
+            g_all[pair, keys_of(side)],
+            (((0,), (0,)), ((), ())),
+            preferred_element_type=jnp.float32,
+        )
+
+    def give_own(w, r):
+        v = w * PARTS + r
+        part_own[v] = partial_own(w, r, other_rep).astype(jnp.bfloat16)
+        send(part_own.at[v], met_own.at[v], 10, e_recv.at[v], across)
+
+    def keep_own(w, r):
+        kept_own[w * PARTS + r] = partial_own(w, r, rep)
+
+    def total_own(w, r):
+        v = w * PARTS + r
+        arrive(met_own.at[v], e_recv.at[v])
+        return kept_own[v] + met_own[v].astype(jnp.float32)
+
+    def turn(r):
+        turned[r] = total_own(1, r).astype(jnp.bfloat16)
+
+    def send_turned(r):
+        send(turned.at[r], got.at[r], 11, f_recv.at[r], shard(base + far))
+
+    for which in (0, 1):
+        keys = keys_of(other_rep if which == 0 else rep)
+        arrive(g_all.at[tokens_of(core), keys], g_recv.at[which, 1])
+    for w in range(2):
+        copies_own[w].wait()
+        arrive(x_own.at[w, mate_tokens], d_recv.at[w])
+    for r in range(PARTS):
+        give_own(1, r)
+
+    @pl.when(inner)
+    def _():
+        pl.semaphore_wait(open_sem, 1)
+        pl.semaphore_signal(open_sem, inc=1, device_id=near, device_id_type=MESH)
 
     chosen = jnp.zeros((blocks, 128), jnp.int32)
     row = lax.broadcasted_iota(jnp.int32, (blocks, 128), 0)
@@ -205,8 +282,16 @@
         ).astype(jnp.bfloat16)
         full = jnp.dot(left, rr[s], preferred_element_type=jnp.float32).astype(jnp.bfloat16)
         prod[:, s] = full.reshape(4, GROUP, height, width)
-    for level in (z_half, z_last, z_near):
-        send(prod.at[level], relay.at[z], 2, u_recv.at[0], shard(level * GROUP + q))
+        if s == 0:
+
+            @pl.when(jnp.logical_not(inner))
+            def _():
+                pl.semaphore_wait(open_sem, 1)
+
+        for level in (z_last, z_half, z_near):
+            send(prod.at[level, s], relay.at[z, s], 2, u_recv.at[0], shard(level * GROUP + q))
+    for r in range(PARTS):
+        give_own(0, r)
     relay[z] = prod[z]
 
     def gather_g(which):
@@ -214,7 +299,6 @@
         view = g_all.at[tokens_of(far), keys]
         arrive(view, g_recv.at[which, 0])
         send(view, view, 0, g_recv.at[which, 2], shard(base + core))
-        arrive(g_all.at[tokens_of(core), keys], g_recv.at[which, 1])
         arrive(g_all.at[tokens_of(both), keys], g_recv.at[which, 2])
 
     def partial(o, r, side):
@@ -243,23 +327,25 @@
         return kept[u] + met[u].astype(jnp.float32)
 
     def pass_near(o, r):
-        u = o * PARTS + r
+        u = o // 2 * PARTS + r
         passed[u] = total_of(o, r).astype(jnp.bfloat16)
         send(passed.at[u], first.at[u], 4, s_recv.at[u], near)
 
     def pass_half(r):
         u = 2 * PARTS + r
-        total = total_of(2, r)
+        total = total_of(1, r)
         arrive(first.at[r], s_recv.at[r])
         passed[u] = (total + first[r].astype(jnp.float32)).astype(jnp.bfloat16)
         send(passed.at[u], second.at[r], 5, t_recv.at[r], opposite)
 
     def finish(r):
-        total = total_of(3, r)
+        total = total_own(0, r)
+        arrive(got.at[r], f_recv.at[r])
+        total = total + got[r].astype(jnp.float32)
+        arrive(second.at[r], t_recv.at[r])
+        total = total + second[r].astype(jnp.float32)
         arrive(first.at[PARTS + r], s_recv.at[PARTS + r])
         total = total + first[PARTS + r].astype(jnp.float32)
-        arrive(second.at[r], t_recv.at[r])
-        total = total + second[r].astype(jnp.float32)
         view = sums.at[rep, unit_of(r)]
         sums[rep, unit_of(r)] = total.astype(jnp.bfloat16)
         send(view, view, 6, r_recv.at[r], across)
@@ -267,17 +353,15 @@
     def slice_of(p):
         return pl.ds(p * piece, piece)
 
-    def spread():
-        arrive(relay.at[pl.ds(0, 3)], u_recv.at[0])
-        for p in range(PIECES):
-            for k, target in ((2, far), (3, both), (1, core)):
-                send(
-                    relay.at[:, :, target, :, slice_of(p)],
-                    upd.at[k, :, :, :, slice_of(p)],
-                    7,
-                    y_recv.at[p],
-                    shard(base + target),
-                )
+    def spread(p):
+        for k, target in ((2, far), (3, both), (1, core)):
+            send(
+                relay.at[:, :, target, :, slice_of(p)],
+                upd.at[k, :, :, :, slice_of(p)],
+                7,
+                y_recv.at[p],
+                shard(base + target),
+            )
 
     def select(p):
         cols = slice(p * piece, (p + 1) * piece)
@@ -294,32 +378,6 @@
         view = rows.at[rep, :, :, slice_of(p)]
         send(view, view, 8, v_recv.at[p], across)
 
-    copy_g.wait()
-    gather_g(0)
-    for o in (0, 1):
-        for r in range(PARTS):
-            give(o, r)
-    gather_g(1)
-    for o in (0, 1):
-        for r in range(PARTS):
-            keep(o, r)
-            pass_near(o, r)
-    give(2, 0)
-    keep(2, 0)
-    give(2, 1)
-    keep(2, 1)
-    spread()
-    give(3, 0)
-    keep(3, 0)
-    pass_half(0)
-    give(3, 1)
-    keep(3, 1)
-    pass_half(1)
-    for r in range(PARTS):
-        finish(r)
-    for p in range(PIECES):
-        select(p)
-
     outs = []
 
     def put(src, dst):
@@ -327,12 +385,54 @@
         copy.start()
         outs.append(copy)
 
-    put(sums.at[rep], og_ref.at[:, keys_of(rep)])
+    def widen(side, r):
+        wide[unit_of(r), keys_of(side)] = sums[side, unit_of(r)].astype(jnp.float32)
+        put(wide.at[unit_of(r), keys_of(side)], og_ref.at[unit_of(r), keys_of(side)])
+
+    for w in (1, 0):
+        for r in range(PARTS):
+            keep_own(w, r)
+    gather_g(0)
+    give(0, 0)
+    give(0, 1)
+    gather_g(1)
+    keep(0, 0)
+    keep(0, 1)
+    pass_near(0, 0)
+    give(1, 0)
+    keep(1, 0)
+    pass_near(0, 1)
+    give(1, 1)
+    keep(1, 1)
+    turn(0)
+    turn(1)
+    give(2, 0)
+    keep(2, 0)
+    arrive(relay.at[pl.ds(0, 3)], u_recv.at[0])
+    spread(0)
+    spread(1)
+    send_turned(0)
+    send_turned(1)
+    spread(2)
+    spread(3)
+    pass_half(0)
+    give(2, 1)
+    keep(2, 1)
+    pass_half(1)
+    pass_near(2, 0)
+    select(0)
+    pass_near(2, 1)
+    select(1)
+    finish(0)
+    finish(1)
+    select(2)
+    select(3)
+    widen(rep, 0)
+    widen(rep, 1)
     put(rows.at[rep], ou_ref.at[rep])
     for r in range(PARTS):
-        view = sums.at[other_rep, unit_of(r)]
-        arrive(view, r_recv.at[r])
-        put(view, og_ref.at[unit_of(r), keys_of(other_rep)])
+        arrive(sums.at[other_rep, unit_of(r)], r_recv.at[r])
+        widen(other_rep, r)
     for p in range(PIECES):
         view = rows.at[other_rep, :, :, slice_of(p)]
         arrive(view, v_recv.at[p])
@@ -341,10 +441,13 @@
     def drain(ref, kind):
         remote(ref, ref, send_sem.at[kind], send_sem.at[kind], across).wait_send()
 
-    drain(x_all.at[pl.ds(0, 3)], 0)
-    drain(x_all.at[pl.ds(0, 3)], 1)
+    drain(x_all, 0)
+    drain(x_all.at[:, pl.ds(0, 3 * tok)], 1)
     drain(relay.at[pl.ds(0, 3)], 2)
     drain(met, 3)
+    drain(prod.at[0], 9)
+    drain(met_own, 10)
+    drain(got, 11)
     drain(met.at[pl.ds(0, 2 * PARTS)], 4)
     drain(met.at[pl.ds(0, PARTS)], 5)
     drain(met.at[pl.ds(0, PARTS)], 6)
@@ -372,13 +475,13 @@
     sums, rows = pl.pallas_call(
         kernel,
         out_shape=(
-            jax.ShapeDtypeStruct((cols, key_width), bf16),
+            jax.ShapeDtypeStruct((cols, key_width), f32),
             jax.ShapeDtypeStruct((n_rep, height, blocks, width), bf16),
         ),
         in_specs=[pl.BlockSpec(memory_space=pltpu.SMEM)] + [any_spec] * 5,
         out_specs=(any_spec, any_spec),
         scratch_shapes=[
-            pltpu.VMEM((4, GROUP * tok, cols), bf16),
+            pltpu.VMEM((3, GROUP * tok, cols), bf16),
             pltpu.VMEM((GROUP * tok, key_width), bf16),
             pltpu.VMEM((slots, n, height, width), bf16),
             pltpu.VMEM(slot_grads.shape, bf16),
@@ -387,27 +490,39 @@
             pltpu.VMEM((4, slots, GROUP, height, width), bf16),
             pltpu.VMEM((4, 4, slots, height, width), bf16),
             pltpu.VMEM((4, height * blocks, per), bf16),
-            pltpu.VMEM((4 * PARTS, unit, half), bf16),
-            pltpu.VMEM((4 * PARTS, unit, half), bf16),
-            pltpu.VMEM((4 * PARTS, unit, half), f32),
+            pltpu.VMEM((3 * PARTS, unit, half), bf16),
+            pltpu.VMEM((3 * PARTS, unit, half), bf16),
+            pltpu.VMEM((3 * PARTS, unit, half), f32),
             pltpu.VMEM((3 * PARTS, unit, half), bf16),
             pltpu.VMEM((2 * PARTS, unit, half), bf16),
             pltpu.VMEM((PARTS, unit, half), bf16),
+            pltpu.VMEM((2, 2 * tok, cols), bf16),
+            pltpu.VMEM((2 * PARTS, unit, half), bf16),
+            pltpu.VMEM((2 * PARTS, unit, half), bf16),
+            pltpu.VMEM((2 * PARTS, unit, half), f32),
+            pltpu.VMEM((PARTS, unit, half), bf16),
+            pltpu.VMEM((PARTS, unit, half), bf16),
             pltpu.VMEM((n_rep, cols, half), bf16),
             pltpu.VMEM((n_rep, height, blocks, width), bf16),
+            pltpu.VMEM((cols, key_width), f32),
+            pltpu.SemaphoreType.REGULAR,
             dma((4,)),
-            dma((4,)),
-            dma((2 + PARTS + PIECES,)),
-            dma((9,)),
+            dma((3,)),
+            dma((1 + 2 * PARTS + PIECES,)),
+            dma((12,)),
             dma((2, 3)),
-            dma((4, PARTS)),
+            dma((3, PARTS)),
             dma((1,)),
             dma((PIECES,)),
-            dma((4 * PARTS,)),
+            dma((3 * PARTS,)),
             dma((2 * PARTS,)),
             dma((PARTS,)),
             dma((PARTS,)),
             dma((PIECES,)),
+            dma((2,)),
+            dma((2,)),
+            dma((2 * PARTS,)),
+            dma((PARTS,)),
         ],
         compiler_params=pltpu.CompilerParams(
             collective_id=0, has_side_effects=True, vmem_limit_bytes=60 * 1024 * 1024
@@ -420,7 +535,7 @@
         slot_grads,
         right_root,
     )
-    return (sums.astype(f32), rows.reshape(n_rep * height, blocks, width))
+    return (sums, rows.reshape(n_rep * height, blocks, width))
 
 
 def shards(tokens_x, key_grad, left_root, slot_grads, right_root, block_slot):

time: 74.2 us -> 64.9 us (0.87)
  Pallas kernels: 70.2 us -> 60.7 us
  local copies, waits for them, and re-layouts: 0.97 us -> 3.37 us
  other arithmetic: 2.21 us -> 0 us
    pallas_call x1, Pallas kernels: 70.2 us -> 60.7 us  [fused_shards(): pl.pallas_call(kernel, out_shape=(jax.ShapeDtypeStruct((cols, key_width),...]
    unnamed x3 -> x4, local copies, waits for them, and re-layouts: 0.97 us -> 3.37 us
    convert_element_type x1 -> x0, other arithmetic: 2.21 us -> none  [fused_shards(): return (sums.astype(f32), rows.reshape(n_rep * height, blocks, width))]
where the time goes in v2:
time: 64.9 us; the launch traced here: 64.7 us
  Pallas kernels  60.7 us (94%)
  local copies, waits for them, and re-layouts  3.37 us (5%)
  between operations  0.65 us (1%)
    pallas_call x1, Pallas kernels, fused_shards(): pl.pallas_call(kernel, out_shape=(jax.ShapeDtypeStruct((cols, key_width),...  60.7 us
    unnamed x4, local copies, waits for them, and re-layouts  3.37 us

profile of v2, /device:TPU:0, one launch (start us, length us, event | category | flops | bytes accessed | tf_op | source)
XLA Modules:
  0.0 64.7 jit_solution(2620980418361556279)
XLA Ops:
  0.6 60.7 %shard_map.77 = (f32[256,1024]{1,0:T(8,128)}, bf16[2,16,32,512]{3,2,1,0:T(8,128)(2,1)}) custom-call(s32[32]{0:T(128)} %slot_ref.1, bf16[256,4096]{1,0:T(8,128)(2,1)} %x_ref.1, bf16[256,1024]{1,0:T(8,128)(2,1)} %g_ref.1, bf16[4,16,2,16,512]{4,3,2,1,0:T(8,128)(2,1)} %bitcast.2, bf16[4,512,512]{2,1,0:T(8,128)(2,1)} %sg_ref.1, bf16[4,512,512]{2,1,0:T(8,128)(2,1)} %rr_ref.1), custom_call_target="tpu_custom_call" | custom-call | tf_op jit(solution)/shard_map/pallas_call | solution.py:475
  61.3 0.0 copy-start
  61.3 2.4 %copy.10 = f32[256,1024]{1,0:T(8,128)} copy(f32[256,1024]{1,0:T(8,128)} %get-tuple-element.8) | data formatting | bytes 2097152
  63.7 0.0 copy-done
  63.7 1.0 %copy.11 = bf16[32,32,512]{2,1,0:T(8,128)(2,1)} copy(bf16[32,32,512]{2,1,0:T(8,128)(2,1)S(1)} %bitcast.3) | data formatting | bytes 2097152
Async XLA Ops:
  61.3 2.4 %copy-start = (bf16[2,16,32,512]{3,2,1,0:T(8,128)(2,1)S(1)}, bf16[2,16,32,512]{3,2,1,0:T(8,128)(2,1)}, u32[]{:S(2)}) copy-start(bf16[2,16,32,512]{3,2,1,0:T(8,128)(2,1)} %get-tuple-element.5) | copy-start | bytes 3145732

commit v3 on v2

--- a/solution.py
+++ b/solution.py
@@ -64,11 +64,11 @@
 
 
 def kernel(
-    slot_ref, x_ref, g_ref, lr_ref, sg_ref, rr_ref, og_ref, ou_ref,
+    where_ref, x_ref, g_ref, lr_ref, sg_ref, rr_ref, wide, rows,
     x_all, g_all, lr, sg, rr, prod, relay, upd, hot, part, met, kept, passed, first, second,
     x_own, part_own, met_own, kept_own, turned, got,
-    sums, rows, wide,
-    open_sem, load_sem, x_load, out_sem, send_sem, g_recv, x_recv, u_recv, y_recv, a_recv, s_recv, t_recv,
+    sums, slot_ref,
+    open_sem, load_sem, slot_load, x_load, send_sem, g_recv, x_recv, u_recv, y_recv, a_recv, s_recv, t_recv,
     r_recv, v_recv, d_load, d_recv, e_recv, f_recv,
 ):
     me = lax.axis_index("shard")
@@ -115,10 +115,16 @@
     def unit_of(r):
         return pl.ds(r * unit, unit)
 
-    copy_lr = pltpu.make_async_copy(lr_ref.at[:, :, rep], lr, load_sem.at[0])
-    copy_sg = pltpu.make_async_copy(sg_ref, sg, load_sem.at[1])
-    copy_rr = pltpu.make_async_copy(rr_ref, rr, load_sem.at[2])
-    copy_g = pltpu.make_async_copy(g_ref, g_all.at[tokens_of(q)], load_sem.at[3])
+    copies_slot = []
+    for s in range(slots):
+        copies_slot.append(
+            (
+                pltpu.make_async_copy(lr_ref.at[s, :, rep], lr.at[s], slot_load.at[s, 0]),
+                pltpu.make_async_copy(sg_ref.at[s], sg.at[s], slot_load.at[s, 1]),
+                pltpu.make_async_copy(rr_ref.at[s], rr.at[s], slot_load.at[s, 2]),
+            )
+        )
+    copy_g = pltpu.make_async_copy(g_ref, g_all.at[tokens_of(q)], load_sem.at[0])
     copies_x = []
     for o in range(3):
         start = pl.multiple_of((order_of[o] * GROUP + q) * (PARTS * unit), 128)
@@ -143,6 +149,7 @@
             )
         )
 
+    copy_g.start()
     barrier = pltpu.get_barrier_semaphore()
     peers = [across, near]
     for index in (core, far, both):
@@ -156,15 +163,18 @@
     def _():
         pl.semaphore_signal(barrier, inc=1, device_id=facing, device_id_type=MESH)
 
-    copy_g.start()
+    copy_slot = pltpu.make_async_copy(where_ref, slot_ref, load_sem.at[1])
+    copy_g.wait()
+    for copy in copies_slot[0]:
+        copy.start()
     for copy in copies_own:
         copy.start()
-    copy_lr.start()
-    copy_sg.start()
-    copy_rr.start()
+    for group in copies_slot[1:]:
+        for copy in group:
+            copy.start()
     for copy in copies_x:
         copy.start()
-    copy_g.wait()
+    copy_slot.start()
     @pl.when(inner)
     def _():
         pl.semaphore_wait(barrier, len(peers) + 1)
@@ -241,20 +251,45 @@
     def send_turned(r):
         send(turned.at[r], got.at[r], 11, f_recv.at[r], shard(base + far))
 
-    for which in (0, 1):
-        keys = keys_of(other_rep if which == 0 else rep)
-        arrive(g_all.at[tokens_of(core), keys], g_recv.at[which, 1])
+    def send_slot(s, levels):
+        for level in levels:
+            send(prod.at[level, s], relay.at[z, s], 2, u_recv.at[0], shard(level * GROUP + q))
+
+    for s in range(slots):
+        for copy in copies_slot[s]:
+            copy.wait()
+        left = jnp.dot(
+            lr[s].reshape(n * height, width), sg[s], preferred_element_type=jnp.float32
+        ).astype(jnp.bfloat16)
+        full = jnp.dot(left, rr[s], preferred_element_type=jnp.float32).astype(jnp.bfloat16)
+        prod[:, s] = full.reshape(4, GROUP, height, width)
+        if s == 0:
+
+            @pl.when(inner)
+            def _():
+                pl.semaphore_wait(open_sem, 1)
+                pl.semaphore_signal(open_sem, inc=1, device_id=near, device_id_type=MESH)
+
+            send_slot(s, (z_near,))
+        elif s == 1:
+
+            @pl.when(jnp.logical_not(inner))
+            def _():
+                pl.semaphore_wait(open_sem, 1)
+
+            send_slot(0, (z_last, z_half))
+            send_slot(1, (z_last, z_half, z_near))
+        else:
+            send_slot(s, (z_last, z_half, z_near))
+
+    arrive(g_all.at[tokens_of(core), keys_of(other_rep)], g_recv.at[0, 1])
     for w in range(2):
         copies_own[w].wait()
         arrive(x_own.at[w, mate_tokens], d_recv.at[w])
     for r in range(PARTS):
         give_own(1, r)
 
-    @pl.when(inner)
-    def _():
-        pl.semaphore_wait(open_sem, 1)
-        pl.semaphore_signal(open_sem, inc=1, device_id=near, device_id_type=MESH)
-
+    copy_slot.wait()
     chosen = jnp.zeros((blocks, 128), jnp.int32)
     row = lax.broadcasted_iota(jnp.int32, (blocks, 128), 0)
     for b in range(blocks):
@@ -273,23 +308,6 @@
                     hit, 1.0, 0.0
                 ).astype(jnp.bfloat16)
 
-    copy_lr.wait()
-    copy_sg.wait()
-    copy_rr.wait()
-    for s in range(slots):
-        left = jnp.dot(
-            lr[s].reshape(n * height, width), sg[s], preferred_element_type=jnp.float32
-        ).astype(jnp.bfloat16)
-        full = jnp.dot(left, rr[s], preferred_element_type=jnp.float32).astype(jnp.bfloat16)
-        prod[:, s] = full.reshape(4, GROUP, height, width)
-        if s == 0:
-
-            @pl.when(jnp.logical_not(inner))
-            def _():
-                pl.semaphore_wait(open_sem, 1)
-
-        for level in (z_last, z_half, z_near):
-            send(prod.at[level, s], relay.at[z, s], 2, u_recv.at[0], shard(level * GROUP + q))
     for r in range(PARTS):
         give_own(0, r)
     relay[z] = prod[z]
@@ -378,17 +396,10 @@
         view = rows.at[rep, :, :, slice_of(p)]
         send(view, view, 8, v_recv.at[p], across)
 
-    outs = []
-
-    def put(src, dst):
-        copy = pltpu.make_async_copy(src, dst, out_sem.at[len(outs)])
-        copy.start()
-        outs.append(copy)
-
     def widen(side, r):
         wide[unit_of(r), keys_of(side)] = sums[side, unit_of(r)].astype(jnp.float32)
-        put(wide.at[unit_of(r), keys_of(side)], og_ref.at[unit_of(r), keys_of(side)])
-
+
+    arrive(g_all.at[tokens_of(core), keys_of(rep)], g_recv.at[1, 1])
     for w in (1, 0):
         for r in range(PARTS):
             keep_own(w, r)
@@ -411,9 +422,9 @@
     arrive(relay.at[pl.ds(0, 3)], u_recv.at[0])
     spread(0)
     spread(1)
+    spread(2)
     send_turned(0)
     send_turned(1)
-    spread(2)
     spread(3)
     pass_half(0)
     give(2, 1)
@@ -423,20 +434,18 @@
     select(0)
     pass_near(2, 1)
     select(1)
+    select(2)
     finish(0)
     finish(1)
-    select(2)
     select(3)
     widen(rep, 0)
     widen(rep, 1)
-    put(rows.at[rep], ou_ref.at[rep])
     for r in range(PARTS):
         arrive(sums.at[other_rep, unit_of(r)], r_recv.at[r])
         widen(other_rep, r)
     for p in range(PIECES):
         view = rows.at[other_rep, :, :, slice_of(p)]
         arrive(view, v_recv.at[p])
-        put(view, ou_ref.at[other_rep, :, :, slice_of(p)])
 
     def drain(ref, kind):
         remote(ref, ref, send_sem.at[kind], send_sem.at[kind], across).wait_send()
@@ -453,7 +462,24 @@
     drain(met.at[pl.ds(0, PARTS)], 6)
     drain(relay.at[pl.ds(0, 3)], 7)
     drain(rows.at[0], 8)
-    for copy in outs:
+
+
+def in_hbm(array):
+    return pltpu.with_memory_space_constraint(array, pltpu.HBM)
+
+
+def in_vmem(array):
+    return pltpu.with_memory_space_constraint(array, pltpu.VMEM)
+
+
+def store(sums_ref, rows_ref, og_ref, ou_ref, sem):
+    copies = (
+        pltpu.make_async_copy(sums_ref, og_ref, sem.at[0]),
+        pltpu.make_async_copy(rows_ref, ou_ref, sem.at[1]),
+    )
+    for copy in copies:
+        copy.start()
+    for copy in copies:
         copy.wait()
 
 
@@ -471,15 +497,16 @@
     per = 4 * slots * height
     bf16, f32 = jnp.bfloat16, jnp.float32
     dma = pltpu.SemaphoreType.DMA
-    any_spec = pl.BlockSpec(memory_space=pl.ANY)
+    hbm_spec = pl.BlockSpec(memory_space=pltpu.HBM)
+    vmem_spec = pl.BlockSpec(memory_space=pltpu.VMEM)
     sums, rows = pl.pallas_call(
         kernel,
         out_shape=(
-            jax.ShapeDtypeStruct((cols, key_width), f32),
-            jax.ShapeDtypeStruct((n_rep, height, blocks, width), bf16),
+            pltpu.VMEM((cols, key_width), f32),
+            pltpu.VMEM((n_rep, height, blocks, width), bf16),
         ),
-        in_specs=[pl.BlockSpec(memory_space=pltpu.SMEM)] + [any_spec] * 5,
-        out_specs=(any_spec, any_spec),
+        in_specs=[hbm_spec] * 6,
+        out_specs=(vmem_spec, vmem_spec),
         scratch_shapes=[
             pltpu.VMEM((3, GROUP * tok, cols), bf16),
             pltpu.VMEM((GROUP * tok, key_width), bf16),
@@ -503,12 +530,11 @@
             pltpu.VMEM((PARTS, unit, half), bf16),
             pltpu.VMEM((PARTS, unit, half), bf16),
             pltpu.VMEM((n_rep, cols, half), bf16),
-            pltpu.VMEM((n_rep, height, blocks, width), bf16),
-            pltpu.VMEM((cols, key_width), f32),
+            pltpu.SMEM(block_slot.shape, jnp.int32),
             pltpu.SemaphoreType.REGULAR,
-            dma((4,)),
+            dma((2,)),
+            dma((slots, 3)),
             dma((3,)),
-            dma((1 + 2 * PARTS + PIECES,)),
             dma((12,)),
             dma((2, 3)),
             dma((3, PARTS)),
@@ -525,17 +551,27 @@
             dma((PARTS,)),
         ],
         compiler_params=pltpu.CompilerParams(
-            collective_id=0, has_side_effects=True, vmem_limit_bytes=60 * 1024 * 1024
+            collective_id=0, has_side_effects=True, vmem_limit_bytes=48 * 1024 * 1024
         ),
     )(
-        block_slot,
-        tokens_x,
-        key_grad,
-        left_root.reshape(slots, n, n_rep, height, width),
-        slot_grads,
-        right_root,
-    )
-    return (sums, rows.reshape(n_rep * height, blocks, width))
+        in_hbm(block_slot),
+        in_hbm(tokens_x),
+        in_hbm(key_grad),
+        in_hbm(left_root.reshape(slots, n, n_rep, height, width)),
+        in_hbm(slot_grads),
+        in_hbm(right_root),
+    )
+    rows = rows.reshape(n_rep * height, blocks, width)
+    return pl.pallas_call(
+        store,
+        out_shape=(
+            jax.ShapeDtypeStruct(sums.shape, sums.dtype),
+            jax.ShapeDtypeStruct(rows.shape, rows.dtype),
+        ),
+        in_specs=[vmem_spec, vmem_spec],
+        out_specs=(hbm_spec, hbm_spec),
+        scratch_shapes=[dma((2,))],
+    )(in_vmem(sums), in_vmem(rows))
 
 
 def shards(tokens_x, key_grad, left_root, slot_grads, right_root, block_slot):
@@ -555,6 +591,7 @@
         and width % (PIECES * 128) == 0
         and per % 128 == 0
         and block_slot.shape[0] % 16 == 0
+        and left_root.shape[0] > 1
     )
     program = fused_shards if aligned else plain_shards
     return program(tokens_x, key_grad, left_root, slot_grads, right_root, block_slot)

time: 64.9 us -> 59.3 us (0.914)
  local copies, waits for them, and re-layouts: 3.37 us -> 0 us
  Pallas kernels: 60.7 us -> 58.5 us
    unnamed x4 -> x0, local copies, waits for them, and re-layouts: 3.37 us -> none
    pallas_call x1 -> x2, Pallas kernels: 60.7 us -> 58.5 us  [the longest x1 57.2 us: fused_shards(): pl.pallas_call(kernel, out_shape=(pltpu.VMEM((cols, key_width), f32), plt...]
where the time goes in v3:
time: 59.3 us; the launch traced here: 59.2 us
  Pallas kernels  58.5 us (99%)
  between operations  0.64 us (1%)
    pallas_call x1, Pallas kernels, fused_shards(): pl.pallas_call(kernel, out_shape=(pltpu.VMEM((cols, key_width), f32), plt...  57.2 us
    pallas_call x1, Pallas kernels, fused_shards(): pl.pallas_call(store, out_shape=(jax.ShapeDtypeStruct(sums.shape, sums.dt...  1.33 us

profile of v3, /device:TPU:0, one launch (start us, length us, event | category | flops | bytes accessed | tf_op | source)
XLA Modules:
  0.0 59.2 jit_solution(11640181471332217684)
XLA Ops:
  0.6 57.2 %shard_map.77 = (f32[256,1024]{1,0:T(8,128)S(1)}, bf16[2,16,32,512]{3,2,1,0:T(8,128)(2,1)S(1)}) custom-call(s32[32]{0:T(128)} %where_ref.1, bf16[256,4096]{1,0:T(8,128)(2,1)} %x_ref.1, bf16[256,1024]{1,0:T(8,128)(2,1)} %g_ref.1, bf16[4,16,2,16,512]{4,3,2,1,0:T(8,128)(2,1)} %bitcast.3, bf16[4,512,512]{2,1,0:T(8,128)(2,1)} %sg_ref.1, bf16[4,512,512]{2,1,0:T(8,128)(2,1)} %rr_ref.1), custom_call_target="tpu_custom_call" | custom-call | tf_op jit(solution)/shard_map/pallas_call | solution.py:502
  57.8 1.3 %shard_map.78 = (f32[256,1024]{1,0:T(8,128)}, bf16[32,32,512]{2,1,0:T(8,128)(2,1)}) custom-call(f32[256,1024]{1,0:T(8,128)S(1)} %get-tuple-element.4.sums_ref, bf16[32,32,512]{2,1,0:T(8,128)(2,1)S(1)} %bitcast.2), custom_call_target="tpu_custom_call" | custom-call | tf_op jit(solution)/shard_map/pallas_call | solution.py:565

commit v4 on v3

--- a/solution.py
+++ b/solution.py
@@ -9,6 +9,7 @@
 GROUP = 4
 PARTS = 2
 PIECES = 4
+HALVES = 2
 
 
 def column_term(features, cotangent):
@@ -377,24 +378,35 @@
                 relay.at[:, :, target, :, slice_of(p)],
                 upd.at[k, :, :, :, slice_of(p)],
                 7,
-                y_recv.at[p],
+                y_recv.at[k // 2, p],
                 shard(base + target),
             )
 
+    lines = height // HALVES
+
     def select(p):
         cols = slice(p * piece, (p + 1) * piece)
-        arrive(upd.at[pl.ds(1, 3), :, :, :, slice_of(p)], y_recv.at[p])
-        value = jnp.dot(
+
+        def block(k):
+            return upd[k, :, :, :, cols].reshape(per, piece)
+
+        arrive(upd.at[1, :, :, :, slice_of(p)], y_recv.at[0, p])
+        early = jnp.dot(
             hot[0], relay[:, :, q, :, cols].reshape(per, piece), preferred_element_type=jnp.float32
-        )
-        for k in range(1, 4):
-            value = value + jnp.dot(
-                hot[k], upd[k, :, :, :, cols].reshape(per, piece),
-                preferred_element_type=jnp.float32,
+        ) + jnp.dot(hot[1], block(1), preferred_element_type=jnp.float32)
+        arrive(upd.at[pl.ds(2, 2), :, :, :, slice_of(p)], y_recv.at[1, p])
+        for h in range(HALVES):
+            here = slice(h * lines * blocks, (h + 1) * lines * blocks)
+            value = early[here]
+            for k in (2, 3):
+                value = value + jnp.dot(
+                    hot[k, here], block(k), preferred_element_type=jnp.float32
+                )
+            rows[rep, h * lines : (h + 1) * lines, :, cols] = value.astype(jnp.bfloat16).reshape(
+                lines, blocks, piece
             )
-        rows[rep, :, :, cols] = value.astype(jnp.bfloat16).reshape(height, blocks, piece)
-        view = rows.at[rep, :, :, slice_of(p)]
-        send(view, view, 8, v_recv.at[p], across)
+            view = rows.at[rep, pl.ds(h * lines, lines), :, slice_of(p)]
+            send(view, view, 8, v_recv.at[p, h], across)
 
     def widen(side, r):
         wide[unit_of(r), keys_of(side)] = sums[side, unit_of(r)].astype(jnp.float32)
@@ -424,8 +436,8 @@
     spread(1)
     spread(2)
     send_turned(0)
+    spread(3)
     send_turned(1)
-    spread(3)
     pass_half(0)
     give(2, 1)
     keep(2, 1)
@@ -436,16 +448,18 @@
     select(1)
     select(2)
     finish(0)
+    select(3)
     finish(1)
-    select(3)
     widen(rep, 0)
     widen(rep, 1)
     for r in range(PARTS):
         arrive(sums.at[other_rep, unit_of(r)], r_recv.at[r])
         widen(other_rep, r)
     for p in range(PIECES):
-        view = rows.at[other_rep, :, :, slice_of(p)]
-        arrive(view, v_recv.at[p])
+        for h in range(HALVES):
+            arrive(
+                rows.at[other_rep, pl.ds(h * lines, lines), :, slice_of(p)], v_recv.at[p, h]
+            )
 
     def drain(ref, kind):
         remote(ref, ref, send_sem.at[kind], send_sem.at[kind], across).wait_send()
@@ -539,12 +553,12 @@
             dma((2, 3)),
             dma((3, PARTS)),
             dma((1,)),
-            dma((PIECES,)),
+            dma((2, PIECES)),
             dma((3 * PARTS,)),
             dma((2 * PARTS,)),
             dma((PARTS,)),
             dma((PARTS,)),
-            dma((PIECES,)),
+            dma((PIECES, HALVES)),
             dma((2,)),
             dma((2,)),
             dma((2 * PARTS,)),

time: 59.3 us -> 59 us (level)
  no operation moved by 1% of the time
where the time goes in v4:
time: 59 us; the launch traced here: 58.8 us
  Pallas kernels  58.2 us (99%)
  between operations  0.64 us (1%)
    pallas_call x1, Pallas kernels, fused_shards(): pl.pallas_call(kernel, out_shape=(pltpu.VMEM((cols, key_width), f32), plt...  56.8 us
    pallas_call x1, Pallas kernels, fused_shards(): pl.pallas_call(store, out_shape=(jax.ShapeDtypeStruct(sums.shape, sums.dt...  1.33 us

profile of v4, /device:TPU:0, one launch (start us, length us, event | category | flops | bytes accessed | tf_op | source)
XLA Modules:
  0.0 58.8 jit_solution(18114611047362162318)
XLA Ops:
  0.6 56.8 %shard_map.77 = (f32[256,1024]{1,0:T(8,128)S(1)}, bf16[2,16,32,512]{3,2,1,0:T(8,128)(2,1)S(1)}) custom-call(s32[32]{0:T(128)} %where_ref.1, bf16[256,4096]{1,0:T(8,128)(2,1)} %x_ref.1, bf16[256,1024]{1,0:T(8,128)(2,1)} %g_ref.1, bf16[4,16,2,16,512]{4,3,2,1,0:T(8,128)(2,1)} %bitcast.3, bf16[4,512,512]{2,1,0:T(8,128)(2,1)} %sg_ref.1, bf16[4,512,512]{2,1,0:T(8,128)(2,1)} %rr_ref.1), custom_call_target="tpu_custom_call" | custom-call | tf_op jit(solution)/shard_map/pallas_call | solution.py:516
  57.5 1.3 %shard_map.78 = (f32[256,1024]{1,0:T(8,128)}, bf16[32,32,512]{2,1,0:T(8,128)(2,1)}) custom-call(f32[256,1024]{1,0:T(8,128)S(1)} %get-tuple-element.4.sums_ref, bf16[32,32,512]{2,1,0:T(8,128)(2,1)S(1)} %bitcast.2), custom_call_target="tpu_custom_call" | custom-call | tf_op jit(solution)/shard_map/pallas_call | solution.py:579

commit v5 on v4

--- a/solution.py
+++ b/solution.py
@@ -208,6 +208,8 @@
             )
 
     send_g(0, far, 0)
+    for r in range(PARTS):
+        send_x(0, r)
     send_g(0, core, 1)
     for w, index in enumerate((core, both)):
         send(
@@ -215,8 +217,6 @@
             shard(base + core),
         )
     send_g(1, core, 1)
-    for r in range(PARTS):
-        send_x(0, r)
     send_g(1, far, 0)
     for o in (1, 2):
         for r in range(PARTS):
@@ -309,8 +309,6 @@
                     hit, 1.0, 0.0
                 ).astype(jnp.bfloat16)
 
-    for r in range(PARTS):
-        give_own(0, r)
     relay[z] = prod[z]
 
     def gather_g(which):
@@ -418,6 +416,8 @@
     gather_g(0)
     give(0, 0)
     give(0, 1)
+    for r in range(PARTS):
+        give_own(0, r)
     gather_g(1)
     keep(0, 0)
     keep(0, 1)

time: 59 us -> 59 us (level)
  no operation moved by 1% of the time
where the time goes in v5:
time: 59 us; the launch traced here: 58.8 us
  Pallas kernels  58.2 us (99%)
  between operations  0.64 us (1%)
    pallas_call x1, Pallas kernels, fused_shards(): pl.pallas_call(kernel, out_shape=(pltpu.VMEM((cols, key_width), f32), plt...  56.8 us
    pallas_call x1, Pallas kernels, fused_shards(): pl.pallas_call(store, out_shape=(jax.ShapeDtypeStruct(sums.shape, sums.dt...  1.33 us

profile of v5, /device:TPU:0, one launch (start us, length us, event | category | flops | bytes accessed | tf_op | source)
XLA Modules:
  0.0 58.8 jit_solution(879380764671556110)
XLA Ops:
  0.6 56.8 %shard_map.77 = (f32[256,1024]{1,0:T(8,128)S(1)}, bf16[2,16,32,512]{3,2,1,0:T(8,128)(2,1)S(1)}) custom-call(s32[32]{0:T(128)} %where_ref.1, bf16[256,4096]{1,0:T(8,128)(2,1)} %x_ref.1, bf16[256,1024]{1,0:T(8,128)(2,1)} %g_ref.1, bf16[4,16,2,16,512]{4,3,2,1,0:T(8,128)(2,1)} %bitcast.3, bf16[4,512,512]{2,1,0:T(8,128)(2,1)} %sg_ref.1, bf16[4,512,512]{2,1,0:T(8,128)(2,1)} %rr_ref.1), custom_call_target="tpu_custom_call" | custom-call | tf_op jit(solution)/shard_map/pallas_call | solution.py:516
  57.5 1.3 %shard_map.78 = (f32[256,1024]{1,0:T(8,128)}, bf16[32,32,512]{2,1,0:T(8,128)(2,1)}) custom-call(f32[256,1024]{1,0:T(8,128)S(1)} %get-tuple-element.4.sums_ref, bf16[32,32,512]{2,1,0:T(8,128)(2,1)S(1)} %bitcast.2), custom_call_target="tpu_custom_call" | custom-call | tf_op jit(solution)/shard_map/pallas_call | solution.py:579
